TPU v7x, 32 devices: a whole 2x2x4 slice. The times are simulated.
32 devices in a mesh: dev: 32 (over z, y, x, core).
Axes of the slice: x: 2, y: 2, z: 4, core: 2. Of those that a mesh axis runs over, the one named last changes fastest.
Arguments:
- state_real: float32 [4194304], P('dev'), may hold values from -24 to 24, as said below
- state_imag: float32 [4194304], P('dev'), may hold values from -24 to 24, as said below
- subsystem: int32 [3], replicated, may hold values from 0 to 16, as said below
Outputs:
- rho_real: float32 [256, 256], P('dev')
- rho_imag: float32 [256, 256], P('dev')
Inputs may be any that keep to these rules, and one draw needn't show every extreme that they name: `subsystem`: the 3 entries are distinct local bit positions in ascending order; the first is always 0 and the last always 17 - 1. `state_real`: real parts of amplitudes; their typical size changes between aligned blocks of 2**(11) local indices by up to a factor of 16. `state_imag`: imaginary parts of amplitudes, with the same block sizes as the real parts.
All inputs are finite; a program needn't handle non-finite values.
Results may differ from a plain program's by a relative error of at most 0.0001.
Values sent between devices are 32-bit elements; how exact they have to be, the bound alone decides.
A program may use at most 192 MiB of HBM per device.

v0:
```python
import functools

import jax
import jax.numpy as jnp
from jax import lax
from jax.experimental import pallas as pl
from jax.experimental.pallas import tpu as pltpu
from jax.sharding import PartitionSpec as P

MESH = pl.DeviceIdType.MESH


def exchange_kernel(n, scale, sub_ref, re_hbm, im_hbm, out_ref, state, mixed, send, recv,
                    part_ref, pair_ref, rows_ref, load_sem, send_sem, recv_sem, own_sem,
                    pair_send, pair_recv, row_send, row_recv):
    me = lax.axis_index("dev")
    barrier = pltpu.get_barrier_semaphore()
    loads = [
        pltpu.make_async_copy(re_hbm, state.at[0], load_sem.at[0]),
        pltpu.make_async_copy(im_hbm, state.at[1], load_sem.at[1]),
    ]
    for load in loads:
        load.start()

    def greet(k, carry):
        pl.semaphore_signal(barrier, inc=1, device_id=(lax.rem(me + k, n),), device_id_type=MESH)
        return carry

    lax.fori_loop(1, n, greet, 0)
    vregs = state.shape[1]
    quarter = vregs // 4
    bits = vregs.bit_length() - 1
    width = vregs // n

    lane = lax.broadcasted_iota(jnp.int32, (8, 128), 1)
    sub = lax.broadcasted_iota(jnp.int32, (8, 128), 0)

    mid = sub_ref[1]
    lane_step = jnp.int32(1)
    for b in range(1, 7):
        lane_step = jnp.where(mid == b, 2**b, lane_step)
    top = 10 + bits - 1
    in_lane = (mid < 7) | (mid == top - 1)
    stride = jnp.int32(vregs // 8)
    for b in range(10, top - 1):
        stride = jnp.where(mid == b, 2 ** (b - 10), stride)
    stride = jnp.where(mid == 7, vregs // 4, stride)
    stride = jnp.where(mid == 9, vregs // 2, stride)
    fixed = mid == 8
    lane_on = jnp.where(in_lane, lane_step, 0)
    lane_hit = jnp.bitwise_and(lane, lane_on) != 0
    lane_keep = lane_hit | (jnp.where(in_lane, 0, 1) != jnp.bitwise_and(lane, 0))
    sub_on = jnp.where(fixed, 0, 2)
    sub_hit = jnp.bitwise_and(sub, sub_on) != 0
    sub_keep = sub_hit | (jnp.where(fixed, 1, 0) != jnp.bitwise_and(sub, 0))

    high4 = sub >= 4
    odd_sub = jnp.bitwise_and(sub, 1) != 0
    odd_lane = jnp.bitwise_and(lane, 1) != 0

    def swap(a, b, hit, keep, step, axis):
        size = (8, 128)[axis]
        back = size - step
        return (
            jnp.where(hit, pltpu.roll(b, step, axis), a),
            jnp.where(keep, b, pltpu.roll(a, back, axis)),
        )

    for load in loads:
        load.wait()

    def first_pass(v, carry):
        for c in range(2):
            x = [state[c, v + quarter * k] for k in range(4)]
            x[0], x[2] = swap(x[0], x[2], high4, high4, 4, 0)
            x[1], x[3] = swap(x[1], x[3], high4, high4, 4, 0)
            for k in (0, 2):
                a, b = swap(x[k], x[k + 1], odd_lane, odd_lane, 1, 1)
                x[k], x[k + 1] = swap(a, b, odd_sub, odd_sub, 1, 0)
            for k in range(4):
                mixed[c, v + quarter * k] = x[k]
        return carry

    lax.fori_loop(0, quarter, first_pass, 0, unroll=4)

    pl.semaphore_wait(barrier, n - 1)

    dests = max(1, 2 // width)
    pairs = max(1, width // 2)
    rounds = n // dests

    def second_pass(k, carry):
        at = lax.rem(me // dests + k, rounds)
        for c in range(2):
            for p in range(pairs):
                u = at * pairs + p
                low = jnp.bitwise_and(u, stride - 1)
                first = 2 * u - low
                a = mixed[c, first]
                b = mixed[c, first + stride]
                a, b = swap(a, b, lane_hit, lane_keep, lane_step, 1)
                a, b = swap(a, b, sub_hit, sub_keep, 2, 0)
                for w, value in enumerate((a, b)):
                    dest, tile = divmod(2 * p + w, width)
                    column = (c * width + tile) * 128
                    send[at * dests + dest, :, column : column + 128] = value
        for e in range(dests):
            j = at * dests + e

            @pl.when(j != me)
            def _():
                pltpu.make_async_remote_copy(
                    src_ref=send.at[j], dst_ref=recv.at[me], send_sem=send_sem,
                    recv_sem=recv_sem, device_id=(j,), device_id_type=MESH,
                ).start()

        return carry

    lax.fori_loop(1, rounds + 1, second_pass, 0)
    own = pltpu.make_async_copy(send.at[me], recv.at[me], own_sem)
    own.start()
    own.wait()
    others = pl.ds(0, n - 1)
    pltpu.make_async_copy(recv.at[others], recv.at[others], recv_sem).wait()

    full = 8 * n
    depth = width * 128
    block = min(full, 256)
    half_blocks = block // 16
    chips = n // 2

    def split(x):
        high = x.astype(jnp.bfloat16)
        return high, (x - high.astype(jnp.float32)).astype(jnp.bfloat16)

    def dot(x, y):
        return lax.dot_general(x, y, (((1,), (1,)), ((), ())), preferred_element_type=jnp.float32)

    right = recv[...].reshape(full, 2 * depth)
    right_h, right_l = split(right)

    def gram_block(i, carry):
        rows = recv[pl.ds(i * (block // 8), block // 8)].reshape(block, 2 * depth)
        turned = jnp.concatenate([rows[:, depth:], -rows[:, :depth]], axis=1)
        for c, left in enumerate((rows, turned)):
            left_h, left_l = split(left)
            result = dot(left_h, right_h) + (dot(left_h, right_l) + dot(left_l, right_h))
            result = result.reshape(half_blocks, 2, 8, full)
            for e in range(2):
                part_ref[e, pl.ds(i * half_blocks, half_blocks), :, c * full : (c + 1) * full] = result[:, e]
        return carry

    lax.fori_loop(0, full // block, gram_block, 0)

    core = lax.rem(me, 2)
    chip = me // 2
    other = 1 - core
    to_pair = pltpu.make_async_remote_copy(
        src_ref=part_ref.at[other], dst_ref=pair_ref, send_sem=pair_send, recv_sem=pair_recv,
        device_id=(2 * chip + other,), device_id_type=MESH,
    )
    to_pair.start()
    to_pair.wait_recv()

    def add_pair(k, carry):
        j = lax.rem(chip + k, chips)
        part_ref[core, j] = part_ref[core, j] + pair_ref[j]

        @pl.when(j != chip)
        def _():
            pltpu.make_async_remote_copy(
                src_ref=part_ref.at[core, j], dst_ref=rows_ref.at[chip], send_sem=row_send,
                recv_sem=row_recv, device_id=(2 * j + core,), device_id_type=MESH,
            ).start()

        return carry

    lax.fori_loop(1, chips + 1, add_pair, 0)
    rows_ref[chip] = part_ref[core, chip]
    rest = pl.ds(0, chips - 1)
    pltpu.make_async_copy(rows_ref.at[rest], rows_ref.at[rest], row_recv).wait()
    out_ref[...] = jnp.sum(rows_ref[...], axis=0) * scale
    pltpu.make_async_copy(send.at[others], send.at[others], send_sem).wait()
    to_pair.wait_send()
    pltpu.make_async_copy(rows_ref.at[rest], rows_ref.at[rest], row_send).wait()


def local(n, state_real, state_imag, subsystem):
    amps = state_real.shape[0]
    vregs = amps // 1024
    width = vregs // n
    full = 8 * n
    chunk = (n, 8, 2 * width * 128)
    out = pl.pallas_call(
        functools.partial(exchange_kernel, n, 8.0 / amps),
        out_shape=jax.ShapeDtypeStruct((8, 2 * full), jnp.float32),
        in_specs=[
            pl.BlockSpec(memory_space=pltpu.SMEM),
            pl.BlockSpec(memory_space=pl.ANY),
            pl.BlockSpec(memory_space=pl.ANY),
        ],
        out_specs=pl.BlockSpec(memory_space=pltpu.VMEM),
        scratch_shapes=[
            pltpu.VMEM((2, vregs, 8, 128), jnp.float32),
            pltpu.VMEM((2, vregs, 8, 128), jnp.float32),
            pltpu.VMEM(chunk, jnp.float32),
            pltpu.VMEM(chunk, jnp.float32),
            pltpu.VMEM((2, n // 2, 8, 2 * full), jnp.float32),
            pltpu.VMEM((n // 2, 8, 2 * full), jnp.float32),
            pltpu.VMEM((n // 2, 8, 2 * full), jnp.float32),
            pltpu.SemaphoreType.DMA((2,)),
        ]
        + [pltpu.SemaphoreType.DMA] * 7,
        compiler_params=pltpu.CompilerParams(
            collective_id=0, has_side_effects=True, vmem_limit_bytes=56 * 2**20
        ),
    )(subsystem, state_real.reshape(vregs, 8, 128), state_imag.reshape(vregs, 8, 128))
    return out[:, :full], out[:, full:]


def solution(mesh):
    return jax.shard_map(
        functools.partial(local, mesh.shape["dev"]),
        mesh=mesh,
        in_specs=(P("dev"), P("dev"), P()),
        out_specs=(P("dev", None), P("dev", None)),
        check_vma=False,
    )
```

profile of v0, /device:TPU:0, one launch (start us, length us, event | category | flops | bytes accessed | tf_op | source)
XLA Modules:
  0.0 46.4 jit_solution(10798314292196369213)
XLA Ops:
  0.6 44.4 %shard_map.50 = f32[8,512]{1,0:T(8,128)} custom-call(s32[3]{0:T(128)} %sub_ref.1, f32[128,8,128]{2,1,0:T(8,128)} %bitcast.2, f32[128,8,128]{2,1,0:T(8,128)} %bitcast.3), custom_call_target="tpu_custom_call" | custom-call | tf_op jit(solution)/shard_map/pallas_call | solution.py:194
  45.1 1.3 %fusion = (f32[8,256]{1,0:T(8,128)}, f32[8,256]{1,0:T(8,128)}) fusion(f32[8,512]{1,0:T(8,128)} %shard_map.50), kind=kLoop, calls=%fused_computation | loop fusion | bytes 32768 | tf_op jit(solution)/shard_map/slice | solution.py:218
where the time goes:
time: 46.6 us; the launch traced here: 46.4 us
  Pallas kernels  44.4 us (95%)
  local copies, waits for them, and re-layouts  1.32 us (3%)
  between operations  0.64 us (1%)
    pallas_call x1, Pallas kernels, local(): pl.pallas_call(functools.partial(exchange_kernel, n, 8.0 / amps), out_sha...  44.4 us
    slice x1, local copies, waits for them, and re-layouts, local(): return (out[:, :full], out[:, full:])  1.32 us

commit v1 on v0

v1 whole, which is shorter than its diff:
```python
import functools

import jax
import jax.numpy as jnp
from jax import lax
from jax.experimental import pallas as pl
from jax.experimental.pallas import tpu as pltpu
from jax.sharding import PartitionSpec as P

MESH = pl.DeviceIdType.MESH


def exchange_kernel(n, scale, sub_hbm, re_hbm, im_hbm, out_ref, sub_ref, state, mixed, send, recv,
                    part_ref, pair_ref, rows_ref, load_sem, send_sem, recv_sem,
                    pair_send, pair_recv, row_send, row_recv):
    me = lax.axis_index("dev")
    barrier = pltpu.get_barrier_semaphore()

    def greet(k, carry):
        pl.semaphore_signal(
            barrier, inc=1, device_id=(jnp.bitwise_xor(me, n - k),), device_id_type=MESH
        )
        return carry

    lax.fori_loop(1, n, greet, 0)
    loads = [
        pltpu.make_async_copy(sub_hbm, sub_ref, load_sem.at[2]),
        pltpu.make_async_copy(re_hbm, state.at[0], load_sem.at[0]),
        pltpu.make_async_copy(im_hbm, state.at[1], load_sem.at[1]),
    ]
    for load in loads:
        load.start()
    vregs = state.shape[1]
    quarter = vregs // 4
    bits = vregs.bit_length() - 1
    width = vregs // n

    for load in loads:
        load.wait()

    lane = lax.broadcasted_iota(jnp.int32, (8, 128), 1)
    sub = lax.broadcasted_iota(jnp.int32, (8, 128), 0)

    mid = sub_ref[1]
    lane_step = jnp.int32(1)
    for b in range(1, 7):
        lane_step = jnp.where(mid == b, 2**b, lane_step)
    top = 10 + bits - 1
    in_lane = (mid < 7) | (mid == top - 1)
    stride = jnp.int32(vregs // 8)
    for b in range(10, top - 1):
        stride = jnp.where(mid == b, 2 ** (b - 10), stride)
    stride = jnp.where(mid == 7, vregs // 4, stride)
    stride = jnp.where(mid == 9, vregs // 2, stride)
    fixed = mid == 8
    lane_on = jnp.where(in_lane, lane_step, 0)
    lane_hit = jnp.bitwise_and(lane, lane_on) != 0
    lane_keep = lane_hit | (jnp.where(in_lane, 0, 1) != jnp.bitwise_and(lane, 0))
    sub_on = jnp.where(fixed, 0, 2)
    sub_hit = jnp.bitwise_and(sub, sub_on) != 0
    sub_keep = sub_hit | (jnp.where(fixed, 1, 0) != jnp.bitwise_and(sub, 0))

    high4 = sub >= 4
    odd_sub = jnp.bitwise_and(sub, 1) != 0
    odd_lane = jnp.bitwise_and(lane, 1) != 0

    def swap(a, b, hit, keep, step, axis):
        size = (8, 128)[axis]
        back = size - step
        return (
            jnp.where(hit, pltpu.roll(b, step, axis), a),
            jnp.where(keep, b, pltpu.roll(a, back, axis)),
        )

    def first_pass(v, carry):
        for c in range(2):
            x = [state[c, v + quarter * k] for k in range(4)]
            x[0], x[2] = swap(x[0], x[2], high4, high4, 4, 0)
            x[1], x[3] = swap(x[1], x[3], high4, high4, 4, 0)
            for k in (0, 2):
                a, b = swap(x[k], x[k + 1], odd_lane, odd_lane, 1, 1)
                x[k], x[k + 1] = swap(a, b, odd_sub, odd_sub, 1, 0)
            for k in range(4):
                mixed[c, v + quarter * k] = x[k]
        return carry

    lax.fori_loop(0, quarter, first_pass, 0, unroll=4)

    dests = max(1, 2 // width)
    pairs = max(1, width // 2)
    rounds = n // dests

    def second_pass(at, carry):
        for c in range(2):
            for p in range(pairs):
                u = at * pairs + p
                low = jnp.bitwise_and(u, stride - 1)
                first = 2 * u - low
                a = mixed[c, first]
                b = mixed[c, first + stride]
                a, b = swap(a, b, lane_hit, lane_keep, lane_step, 1)
                a, b = swap(a, b, sub_hit, sub_keep, 2, 0)
                for w, value in enumerate((a, b)):
                    dest, tile = divmod(2 * p + w, width)
                    column = (c * width + tile) * 128
                    send[at * dests + dest, :, column : column + 128] = value
        return carry

    lax.fori_loop(0, rounds, second_pass, 0, unroll=4)

    core = lax.rem(me, 2)
    other = 1 - core
    chip = me // 2
    chips = n // 2
    pl.semaphore_wait(barrier, n - 1)

    def send_chunk(k, carry):
        j = jnp.bitwise_xor(me, n - k)
        pltpu.make_async_remote_copy(
            src_ref=send.at[j], dst_ref=recv.at[chip, core], send_sem=send_sem,
            recv_sem=recv_sem, device_id=(j,), device_id_type=MESH,
        ).start()
        return carry

    lax.fori_loop(1, n, send_chunk, 0)
    pltpu.make_async_copy(send.at[me], recv.at[chip, core], recv_sem).start()
    pltpu.make_async_copy(recv, recv, recv_sem).wait()

    full = 8 * n
    depth = width * 128
    block = min(full // 2, 256)
    blocks = full // 2 // block
    group = block // 8

    def split(x):
        high = x.astype(jnp.bfloat16)
        return high, (x - high.astype(jnp.float32)).astype(jnp.bfloat16)

    def dot(x, y):
        return lax.dot_general(x, y, (((1,), (1,)), ((), ())), preferred_element_type=jnp.float32)

    right_h, right_l = split(recv[...].reshape(full, 2 * depth))

    def gram(side):
        def gram_block(i, carry):
            chunk = pl.ds(i * group, group)
            left = recv[chunk, side].reshape(block, 2 * depth)
            turned = jnp.concatenate([left[:, depth:], -left[:, :depth]], axis=1)
            left_h, left_l = split(jnp.concatenate([left, turned], axis=0))
            result = dot(left_h, right_h) + (dot(left_h, right_l) + dot(left_l, right_h))
            for c in range(2):
                part_ref[side, chunk, :, c * full : (c + 1) * full] = result[
                    c * block : (c + 1) * block
                ].reshape(group, 8, full)
            return carry

        lax.fori_loop(0, blocks, gram_block, 0)

    to_pair = pltpu.make_async_remote_copy(
        src_ref=part_ref.at[other], dst_ref=pair_ref, send_sem=pair_send, recv_sem=pair_recv,
        device_id=(2 * chip + other,), device_id_type=MESH,
    )
    gram(other)
    to_pair.start()
    gram(core)
    to_pair.wait_recv()

    def add_pair(k, carry):
        j = jnp.bitwise_xor(chip, chips - k)
        part_ref[core, j] = part_ref[core, j] + pair_ref[j]
        pltpu.make_async_remote_copy(
            src_ref=part_ref.at[core, j], dst_ref=rows_ref.at[chip], send_sem=row_send,
            recv_sem=row_recv, device_id=(2 * j + core,), device_id_type=MESH,
        ).start()
        return carry

    lax.fori_loop(1, chips, add_pair, 0)
    rows_ref[chip] = part_ref[core, chip] + pair_ref[chip]
    rest = pl.ds(0, chips - 1)
    pltpu.make_async_copy(rows_ref.at[rest], rows_ref.at[rest], row_recv).wait()
    out_ref[...] = jnp.sum(rows_ref[...], axis=0) * scale
    others = send.at[pl.ds(0, n - 1)]
    pltpu.make_async_copy(others, others, send_sem).wait()
    to_pair.wait_send()
    pltpu.make_async_copy(rows_ref.at[rest], rows_ref.at[rest], row_send).wait()


def local(n, state_real, state_imag, subsystem):
    amps = state_real.shape[0]
    vregs = amps // 1024
    width = vregs // n
    full = 8 * n
    chunk = (n, 8, 2 * width * 128)
    out = pl.pallas_call(
        functools.partial(exchange_kernel, n, 8.0 / amps),
        out_shape=jax.ShapeDtypeStruct((8, 2 * full), jnp.float32),
        in_specs=[
            pl.BlockSpec(memory_space=pl.ANY),
            pl.BlockSpec(memory_space=pl.ANY),
            pl.BlockSpec(memory_space=pl.ANY),
        ],
        out_specs=pl.BlockSpec(memory_space=pltpu.VMEM),
        scratch_shapes=[
            pltpu.SMEM((3,), jnp.int32),
            pltpu.VMEM((2, vregs, 8, 128), jnp.float32),
            pltpu.VMEM((2, vregs, 8, 128), jnp.float32),
            pltpu.VMEM(chunk, jnp.float32),
            pltpu.VMEM((n // 2, 2) + chunk[1:], jnp.float32),
            pltpu.VMEM((2, n // 2, 8, 2 * full), jnp.float32),
            pltpu.VMEM((n // 2, 8, 2 * full), jnp.float32),
            pltpu.VMEM((n // 2, 8, 2 * full), jnp.float32),
            pltpu.SemaphoreType.DMA((3,)),
        ]
        + [pltpu.SemaphoreType.DMA] * 6,
        compiler_params=pltpu.CompilerParams(
            collective_id=0, has_side_effects=True, vmem_limit_bytes=56 * 2**20
        ),
    )(subsystem, state_real.reshape(vregs, 8, 128), state_imag.reshape(vregs, 8, 128))
    return out[:, :full], out[:, full:]


def solution(mesh):
    return jax.shard_map(
        functools.partial(local, mesh.shape["dev"]),
        mesh=mesh,
        in_specs=(P("dev"), P("dev"), P()),
        out_specs=(P("dev", None), P("dev", None)),
        check_vma=False,
    )
```

time: 46.6 us -> 41.5 us (0.89)
  Pallas kernels: 44.4 us -> 39.3 us
    pallas_call x1, Pallas kernels: 44.4 us -> 39.3 us  [local(): pl.pallas_call(functools.partial(exchange_kernel, n, 8.0 / amps), out_sha...]
where the time goes in v1:
time: 41.5 us; the launch traced here: 41.3 us
  Pallas kernels  39.3 us (95%)
  local copies, waits for them, and re-layouts  1.32 us (3%)
  between operations  0.64 us (2%)
    pallas_call x1, Pallas kernels, local(): pl.pallas_call(functools.partial(exchange_kernel, n, 8.0 / amps), out_sha...  39.3 us
    slice x1, local copies, waits for them, and re-layouts, local(): return (out[:, :full], out[:, full:])  1.32 us

profile of v1, /device:TPU:0, one launch (start us, length us, event | category | flops | bytes accessed | tf_op | source)
XLA Modules:
  0.0 41.3 jit_solution(12981866682367136727)
XLA Ops:
  0.6 39.3 %shard_map.50 = f32[8,512]{1,0:T(8,128)} custom-call(s32[3]{0:T(128)} %sub_hbm.1, f32[128,8,128]{2,1,0:T(8,128)} %bitcast.2, f32[128,8,128]{2,1,0:T(8,128)} %bitcast.3), custom_call_target="tpu_custom_call" | custom-call | tf_op jit(solution)/shard_map/pallas_call | solution.py:194
  39.9 1.3 %fusion = (f32[8,256]{1,0:T(8,128)}, f32[8,256]{1,0:T(8,128)}) fusion(f32[8,512]{1,0:T(8,128)} %shard_map.50), kind=kLoop, calls=%fused_computation | loop fusion | bytes 32768 | tf_op jit(solution)/shard_map/slice | solution.py:219

commit v2 on v1

--- a/solution.py
+++ b/solution.py
@@ -10,8 +10,8 @@
 MESH = pl.DeviceIdType.MESH
 
 
-def exchange_kernel(n, scale, sub_hbm, re_hbm, im_hbm, out_ref, sub_ref, state, mixed, send, recv,
-                    part_ref, pair_ref, rows_ref, load_sem, send_sem, recv_sem,
+def exchange_kernel(n, sub_hbm, re_hbm, im_hbm, rows_ref, sub_ref, state, mixed, send, recv,
+                    part_ref, pair_ref, load_sem, send_sem, recv_sem,
                     pair_send, pair_recv, row_send, row_recv):
     me = lax.axis_index("dev")
     barrier = pltpu.get_barrier_semaphore()
@@ -175,10 +175,10 @@
         return carry
 
     lax.fori_loop(1, chips, add_pair, 0)
-    rows_ref[chip] = part_ref[core, chip] + pair_ref[chip]
+    part_ref[core, chip] = part_ref[core, chip] + pair_ref[chip]
+    pltpu.make_async_copy(part_ref.at[core, chip], rows_ref.at[chip], row_recv).start()
     rest = pl.ds(0, chips - 1)
-    pltpu.make_async_copy(rows_ref.at[rest], rows_ref.at[rest], row_recv).wait()
-    out_ref[...] = jnp.sum(rows_ref[...], axis=0) * scale
+    pltpu.make_async_copy(rows_ref, rows_ref, row_recv).wait()
     others = send.at[pl.ds(0, n - 1)]
     pltpu.make_async_copy(others, others, send_sem).wait()
     to_pair.wait_send()
@@ -192,14 +192,14 @@
     full = 8 * n
     chunk = (n, 8, 2 * width * 128)
     out = pl.pallas_call(
-        functools.partial(exchange_kernel, n, 8.0 / amps),
-        out_shape=jax.ShapeDtypeStruct((8, 2 * full), jnp.float32),
+        functools.partial(exchange_kernel, n),
+        out_shape=jax.ShapeDtypeStruct((n // 2, 8, 2 * full), jnp.float32),
         in_specs=[
             pl.BlockSpec(memory_space=pl.ANY),
             pl.BlockSpec(memory_space=pl.ANY),
             pl.BlockSpec(memory_space=pl.ANY),
         ],
-        out_specs=pl.BlockSpec(memory_space=pltpu.VMEM),
+        out_specs=pl.BlockSpec(memory_space=pl.ANY),
         scratch_shapes=[
             pltpu.SMEM((3,), jnp.int32),
             pltpu.VMEM((2, vregs, 8, 128), jnp.float32),
@@ -208,7 +208,6 @@
             pltpu.VMEM((n // 2, 2) + chunk[1:], jnp.float32),
             pltpu.VMEM((2, n // 2, 8, 2 * full), jnp.float32),
             pltpu.VMEM((n // 2, 8, 2 * full), jnp.float32),
-            pltpu.VMEM((n // 2, 8, 2 * full), jnp.float32),
             pltpu.SemaphoreType.DMA((3,)),
         ]
         + [pltpu.SemaphoreType.DMA] * 6,
@@ -216,7 +215,8 @@
             collective_id=0, has_side_effects=True, vmem_limit_bytes=56 * 2**20
         ),
     )(subsystem, state_real.reshape(vregs, 8, 128), state_imag.reshape(vregs, 8, 128))
-    return out[:, :full], out[:, full:]
+    total = jnp.sum(out, axis=0) * (8.0 / amps)
+    return total[:, :full], total[:, full:]
 
 
 def solution(mesh):

time: 41.5 us -> 41.2 us (level)
  other arithmetic: 0 us -> 0.98 us
  local copies, waits for them, and re-layouts: 1.32 us -> 0.61 us
  Pallas kernels: 39.3 us -> 38.8 us
    reduce_sum x0 -> x1, other arithmetic: none -> 0.98 us  [local(): total = jnp.sum(out, axis=0) * (8.0 / amps)]
    slice x1, local copies, waits for them, and re-layouts: 1.32 us -> 0.61 us  [local(): return (total[:, :full], total[:, full:])]
    pallas_call x1, Pallas kernels: 39.3 us -> 38.8 us  [local(): pl.pallas_call(functools.partial(exchange_kernel, n), out_shape=jax.Shape...]
where the time goes in v2:
time: 41.2 us; the launch traced here: 41 us
  Pallas kernels  38.8 us (94%)
  other arithmetic  0.98 us (2%)
  between operations  0.65 us (2%)
  local copies, waits for them, and re-layouts  0.61 us (1%)
    pallas_call x1, Pallas kernels, local(): pl.pallas_call(functools.partial(exchange_kernel, n), out_shape=jax.Shape...  38.8 us
    reduce_sum x1, other arithmetic, local(): total = jnp.sum(out, axis=0) * (8.0 / amps)  0.98 us

profile of v2, /device:TPU:0, one launch (start us, length us, event | category | flops | bytes accessed | tf_op | source)
XLA Modules:
  0.0 41.0 jit_solution(652814598960583497)
XLA Ops:
  0.6 38.8 %shard_map.50 = f32[16,8,512]{2,1,0:T(8,128)} custom-call(s32[3]{0:T(128)} %sub_hbm.1, f32[128,8,128]{2,1,0:T(8,128)} %bitcast.2, f32[128,8,128]{2,1,0:T(8,128)} %bitcast.3), custom_call_target="tpu_custom_call" | custom-call | tf_op jit(solution)/shard_map/pallas_call | solution.py:194
  39.4 1.0 %reduce_sum.9 = f32[8,512]{1,0:T(8,128)S(1)} reduce(f32[16,8,512]{2,1,0:T(8,128)} %shard_map.50, f32[]{:T(128)} %constant.0.clone.1), dimensions={0}, to_apply=%region_0.0 | reduce | flops 61440 | bytes 278532 | tf_op jit(solution)/shard_map/reduce_sum | solution.py:218
  40.4 0.6 %fusion = (f32[8,256]{1,0:T(8,128)}, f32[8,256]{1,0:T(8,128)}) fusion(f32[8,512]{1,0:T(8,128)S(1)} %broadcast_multiply_fusion), kind=kLoop, calls=%fused_computation.1 | loop fusion | bytes 32768 | tf_op jit(solution)/shard_map/slice | solution.py:219
  (1 shorter events, 0.0 us)
